TPU v7x, 128 devices: a whole 4x4x4 slice. The times are simulated.
128 devices in a mesh: walk: 8 (over y, x_lo), orb: 16 (over x_hi, z, core).
Axes of the slice: x: 4 (x_hi: 2, x_lo: 2; x = x_hi * 2 + x_lo), y: 4, z: 4, core: 2. Of those that a mesh axis runs over, the one named last changes fastest.
Arguments:
- coefficients: bfloat16 [4096, 4096], P(None, 'orb'), may hold values from -6 to 6
- inverse: bfloat16 [8, 1024, 1024], P('walk', 'orb'), may hold values from -0.005859375 to 0.005859375
- cell_index: int32 [8, 3, 1024], P('walk'), may hold values from 0 to 15
- fraction: float32 [8, 3, 1024], P('walk'), may hold values from 0 to 1
- energies: float32 [8], P('walk'), may hold values from -8 to 8
- weights: float32 [8], P('walk'), may hold values from 0.5 to 2
- occupied: int32 [1024], replicated, may hold values from 0 to 4095, as said below
Outputs:
- gradient: float32 [1024, 4096], P('walk', 'orb')
Inputs may be any that keep to these rules, and one draw needn't show every extreme that they name: `occupied`: 1024 distinct orbital indices; every block of 256 consecutive orbital indices holds at most 96 of them, and some block holds exactly 96.
All inputs are finite; a program needn't handle non-finite values.
Results may differ from a plain program's by a relative error of at most 0.019.
Values may be sent and summed in bfloat16 or wider, within the bound.
A program may use at most 64 MiB of HBM per device.

v0:
```python
import jax
import jax.numpy as jnp
from jax import lax
from jax.sharding import PartitionSpec as P

GRID = 16


def joined_along(blocks, dim):
    dims = list(blocks.shape[1:])
    dims[dim] *= blocks.shape[0]
    return jnp.moveaxis(blocks, 0, dim).reshape(dims)


def work_in_pieces(shard, axis, dim, work, out_dim):
    span = shard.shape[dim]
    pieces = jnp.split(shard, 2, axis=dim) if span % 2 == 0 else [shard]
    first = jnp.arange(lax.axis_size(axis)) * span
    blocks = [lax.all_gather(slab, axis) for slab in pieces]
    made = [jax.vmap(work)(b, first + k * (span // len(pieces))) for k, b in enumerate(blocks)]
    return joined_along(jnp.concatenate(made, axis=out_dim + 1), out_dim)


def split_up(shard, dim, size):
    before, after = (shard.shape[:dim], shard.shape[dim + 1 :])
    return jnp.moveaxis(shard.reshape(*before, size, -1, *after), dim, 0)


def summed_on_arrival(shard, axis, dim):
    size = lax.axis_size(axis)
    blocks = lax.all_to_all(split_up(shard, dim, size), axis, 0, 0, tiled=True)
    return jnp.sum(blocks.astype(jnp.float32), axis=0)


def spline_basis(frac):
    remain = 1.0 - frac
    square = frac * frac
    cubed = square * frac
    values = (
        jnp.stack(
            [
                remain * remain * remain,
                3.0 * cubed - 6.0 * square + 4.0,
                -3.0 * cubed + 3.0 * square + 3.0 * frac + 1.0,
                cubed,
            ]
        )
        / 6.0
    )
    curves = jnp.stack([remain, 3.0 * frac - 2.0, 1.0 - 3.0 * frac, frac])
    return (values, curves)


def evaluate(coefficients, cell_one, frac_one, edge):
    shifts = jnp.arange(4, dtype=jnp.int32)[:, None] - 1
    index_x = (cell_one[0][None, :] + shifts) % edge
    index_y = (cell_one[1][None, :] + shifts) % edge
    index_z = (cell_one[2][None, :] + shifts) % edge
    value_x, curve_x = spline_basis(frac_one[0])
    value_y, curve_y = spline_basis(frac_one[1])
    value_z, curve_z = spline_basis(frac_one[2])
    plane = (index_y[:, None, :] * edge + index_z[None, :, :]).reshape(16, -1)
    value_yz = (value_y[:, None, :] * value_z[None, :, :]).reshape(16, -1)
    curve_yz = (
        curve_y[:, None, :] * value_z[None, :, :] + value_y[:, None, :] * curve_z[None, :, :]
    ).reshape(16, -1)
    electrons = cell_one.shape[1]
    orb_width = coefficients.shape[1]
    all_rows = (index_x[:, None, :] * (edge * edge) + plane[None, :, :]).reshape(64, electrons)
    weight_val = (value_x[:, None, :] * value_yz[None, :, :]).reshape(64, electrons)
    weight_lap = (
        curve_x[:, None, :] * value_yz[None, :, :] + value_x[:, None, :] * curve_yz[None, :, :]
    ).reshape(64, electrons)
    val_high = weight_val.astype(jnp.bfloat16)
    val_low = (weight_val - val_high.astype(jnp.float32)).astype(jnp.bfloat16)
    lap_high = weight_lap.astype(jnp.bfloat16)
    lap_low = (weight_lap - lap_high.astype(jnp.float32)).astype(jnp.bfloat16)
    stacked = jnp.stack([val_high, val_low, lap_high, lap_low])
    block = 256
    count = electrons // block
    rows_blocked = jnp.transpose(all_rows.reshape(64, count, block), (1, 2, 0))
    weights_blocked = jnp.transpose(stacked.reshape(4, 64, count, block), (2, 3, 0, 1))

    def one_block(items):
        rows_one, weights_one = items
        gathered = jnp.take(coefficients, rows_one, axis=0)
        parts = jnp.einsum(
            "nqk,nkw->nqw", weights_one, gathered, preferred_element_type=jnp.float32
        )
        orbital_sum = parts[:, 0, :] + parts[:, 1, :]
        laplace_sum = parts[:, 2, :] + parts[:, 3, :]
        return jnp.concatenate(
            [orbital_sum.astype(jnp.bfloat16), laplace_sum.astype(jnp.bfloat16)], axis=1
        )

    results = lax.map(one_block, (rows_blocked, weights_blocked))
    return results.reshape(electrons, 2 * orb_width)


def apply_inverse(inverse_rows, both_vals):

    def multiply(inv_piece, first_row):
        return jnp.dot(inv_piece, both_vals, preferred_element_type=jnp.float32)

    return work_in_pieces(inverse_rows, "orb", 0, multiply, 0)


def slot_tables(occupied, shard_index, orb_width, capacity):
    mine = occupied // orb_width == shard_index
    ranking = jnp.cumsum(mine.astype(jnp.int32)) - 1
    slot_ids = jnp.arange(capacity, dtype=jnp.int32)
    placed = mine[None, :] & (ranking[None, :] == slot_ids[:, None])
    positions = jnp.arange(occupied.shape[0], dtype=jnp.int32)
    slot_rows = jnp.sum(jnp.where(placed, positions[None, :], 0), axis=1)
    local_cols = occupied - shard_index * orb_width
    slot_cols = jnp.sum(jnp.where(placed, local_cols[None, :], 0), axis=1)
    filled = jnp.any(placed, axis=1)
    picker = (
        (jnp.arange(orb_width, dtype=jnp.int32)[:, None] == slot_cols[None, :]) & filled[None, :]
    ).astype(jnp.bfloat16)
    return (picker, slot_rows)


def couple_slots(kinetic_low, ratio, picker, slot_rows):
    slot_block = jnp.einsum(
        "ls,nl->sn", picker, kinetic_low, preferred_element_type=jnp.float32
    ).astype(jnp.bfloat16)
    ratio_rows = jnp.take(ratio, lax.all_gather(slot_rows, "orb", axis=0, tiled=True), axis=0)
    return jnp.einsum(
        "sn,sw->nw",
        lax.all_gather(slot_block, "orb", axis=0, tiled=True),
        ratio_rows,
        preferred_element_type=jnp.float32,
    )


def body(coefficients, inverse, cell_index, fraction, energies, weights, occupied):
    orb_width = coefficients.shape[1]
    orb_count = lax.axis_size("orb")
    shard_index = lax.axis_index("orb")
    electrons = occupied.shape[0]
    capacity = 3 * electrons // (2 * orb_count)
    picker, slot_rows = slot_tables(occupied, shard_index, orb_width, capacity)
    running = jnp.zeros((electrons, orb_width), jnp.float32)

    def finish(running, products, energy, weight):
        ratio = products[:, :orb_width].astype(jnp.bfloat16)
        kinetic = products[:, orb_width:]
        kinetic_low = kinetic.astype(jnp.bfloat16)
        coupled = couple_slots(kinetic_low, ratio, picker, slot_rows)
        sample_term = weight * (energy * ratio.astype(jnp.float32) - 0.5 * (kinetic - coupled))
        return running + sample_term

    def step_each(running, items):
        inverse_one, cells_one, frac_one, energy, weight = items
        products = apply_inverse(inverse_one, evaluate(coefficients, cells_one, frac_one, GRID))
        return (finish(running, products, energy, weight), None)

    running, unused = lax.scan(
        step_each, running, (inverse, cell_index, fraction, energies, weights)
    )
    return summed_on_arrival(running.astype(jnp.bfloat16), "walk", 0)


def solution(mesh):
    in_specs = (
        P(None, "orb"),
        P("walk", "orb", None),
        P("walk", None, None),
        P("walk", None, None),
        P("walk"),
        P("walk"),
        P(),
    )
    out_specs = P("walk", "orb")
    return jax.shard_map(body, mesh=mesh, in_specs=in_specs, out_specs=out_specs, check_vma=False)
```

profile of v0, /device:TPU:0, one launch (start us, length us, event | category | flops | bytes accessed | tf_op | source)
XLA Modules:
  0.0 392.6 jit_solution(9786935563459408953)
XLA Ops:
  6.5 1.7 fusion.39
  8.3 0.7 all-gather.4.cloned.1.call-update
  9.0 0.8 fusion.28
  9.8 0.8 broadcast_subtract_fusion.3
  10.9 0.1 add.378
  11.0 0.1 subtract_convert_fusion
  11.1 0.1 mul.535
  11.2 0.1 subtract_convert_fusion.1
  11.3 0.1 fusion.23
  11.5 0.1 add.399
  11.7 0.5 maximum_bitcast_fusion.1
  12.2 294.5 %while.17 = (s32[]{:T(128)}, bf16[4,256,512]{2,1,0:T(8,128)(2,1)}, bf16[4,256,4,64]{1,0,3,2:T(4,128)(2,1)S(1)}, s32[4,256,64]{1,0,2:T(4,128)S(1)}, bf16[4096,256]{1,0:T(8,128)(2,1)S(1)}, /*index=5*/s32[]{:T(128)}) while((s32[]{:T(128)}, bf16[4,256,512]{2,1,0:T(8,128)(2,1)}, bf16[4,256,4,64]{1,0,3,2:T(4,128)(2,1)S(1)}, ...), condition=%wide.region_1.2_spmd, body=%wide.region_0.1_spmd.sunk | while | flops 38699008 | bytes 30048844 | solution.py:96
  12.2 0.1 constant_dynamic-slice_fusion.4
  12.2 0.1 copy.28
  12.4 0.1 reshape.712
  12.5 64.8 %gather_fusion = bf16[16384,256]{1,0:T(8,128)(2,1)} fusion(bf16[4096,256]{1,0:T(8,128)(2,1)S(1)} %get-tuple-element.202, s32[16384]{0:T(1024)S(1)} %broadcast_clamp_fusion.2), kind=kCustom, calls=%fused_computation.clone.1 | custom fusion | bytes 16842752 | tf_op jit(solution)/shard_map/while/body/eval_jaxpr/while/body/eval_jaxpr/jit(_take)/gather | solution.py:86
  77.4 0.3 constant_dynamic-slice_fusion.5
  77.7 0.2 copy.29
  77.9 6.5 %fusion.53 = f32[256,4,256]{2,1,0:T(4,128)S(1)} fusion(bf16[256,64,256]{2,1,0:T(8,128)(2,1)} %bitcast.100, pred[256,64]{1,0:T(8,128)(4,1)S(1)} %compare_and_fusion.3, bf16[1,256,4,64]{3,2,1,0:T(4,128)(2,1)S(1)} %copy.29), kind=kOutput, calls=%fused_computation.2.clone.1 | convolution fusion | flops 37748736 | bytes 9584640 | tf_op jit(solution)/shard_map/while/body/eval_jaxpr/while/body/eval_jaxpr/nqk,nkw->nqw/dot_general | solution.py:87
  84.3 0.7 fusion.54
  85.1 0.7 fusion.55
  85.9 0.1 copy.28
  86.0 0.1 reshape.712
  86.1 64.8 %gather_fusion = bf16[16384,256]{1,0:T(8,128)(2,1)} fusion(bf16[4096,256]{1,0:T(8,128)(2,1)S(1)} %get-tuple-element.202, s32[16384]{0:T(1024)S(1)} %broadcast_clamp_fusion.2), kind=kCustom, calls=%fused_computation.clone.1 | custom fusion | bytes 16842752 | tf_op jit(solution)/shard_map/while/body/eval_jaxpr/while/body/eval_jaxpr/jit(_take)/gather | solution.py:86
  151.0 0.3 constant_dynamic-slice_fusion.5
  151.3 0.2 copy.29
  151.5 6.5 %fusion.53 = f32[256,4,256]{2,1,0:T(4,128)S(1)} fusion(bf16[256,64,256]{2,1,0:T(8,128)(2,1)} %bitcast.100, pred[256,64]{1,0:T(8,128)(4,1)S(1)} %compare_and_fusion.3, bf16[1,256,4,64]{3,2,1,0:T(4,128)(2,1)S(1)} %copy.29), kind=kOutput, calls=%fused_computation.2.clone.1 | convolution fusion | flops 37748736 | bytes 9584640 | tf_op jit(solution)/shard_map/while/body/eval_jaxpr/while/body/eval_jaxpr/nqk,nkw->nqw/dot_general | solution.py:87
  158.0 0.7 fusion.54
  158.7 0.7 fusion.55
  159.5 0.1 copy.28
  159.6 0.1 reshape.712
  159.7 64.8 %gather_fusion = bf16[16384,256]{1,0:T(8,128)(2,1)} fusion(bf16[4096,256]{1,0:T(8,128)(2,1)S(1)} %get-tuple-element.202, s32[16384]{0:T(1024)S(1)} %broadcast_clamp_fusion.2), kind=kCustom, calls=%fused_computation.clone.1 | custom fusion | bytes 16842752 | tf_op jit(solution)/shard_map/while/body/eval_jaxpr/while/body/eval_jaxpr/jit(_take)/gather | solution.py:86
  224.6 0.3 constant_dynamic-slice_fusion.5
  224.9 0.2 copy.29
  225.1 6.5 %fusion.53 = f32[256,4,256]{2,1,0:T(4,128)S(1)} fusion(bf16[256,64,256]{2,1,0:T(8,128)(2,1)} %bitcast.100, pred[256,64]{1,0:T(8,128)(4,1)S(1)} %compare_and_fusion.3, bf16[1,256,4,64]{3,2,1,0:T(4,128)(2,1)S(1)} %copy.29), kind=kOutput, calls=%fused_computation.2.clone.1 | convolution fusion | flops 37748736 | bytes 9584640 | tf_op jit(solution)/shard_map/while/body/eval_jaxpr/while/body/eval_jaxpr/nqk,nkw->nqw/dot_general | solution.py:87
  231.6 0.7 fusion.54
  232.3 0.7 fusion.55
  233.1 0.1 copy.28
  233.2 0.1 reshape.712
  233.3 64.8 %gather_fusion = bf16[16384,256]{1,0:T(8,128)(2,1)} fusion(bf16[4096,256]{1,0:T(8,128)(2,1)S(1)} %get-tuple-element.202, s32[16384]{0:T(1024)S(1)} %broadcast_clamp_fusion.2), kind=kCustom, calls=%fused_computation.clone.1 | custom fusion | bytes 16842752 | tf_op jit(solution)/shard_map/while/body/eval_jaxpr/while/body/eval_jaxpr/jit(_take)/gather | solution.py:86
  298.2 0.3 constant_dynamic-slice_fusion.5
  298.5 0.2 copy.29
  298.7 6.5 %fusion.53 = f32[256,4,256]{2,1,0:T(4,128)S(1)} fusion(bf16[256,64,256]{2,1,0:T(8,128)(2,1)} %bitcast.100, pred[256,64]{1,0:T(8,128)(4,1)S(1)} %compare_and_fusion.3, bf16[1,256,4,64]{3,2,1,0:T(4,128)(2,1)S(1)} %copy.29), kind=kOutput, calls=%fused_computation.2.clone.1 | convolution fusion | flops 37748736 | bytes 9584640 | tf_op jit(solution)/shard_map/while/body/eval_jaxpr/while/body/eval_jaxpr/nqk,nkw->nqw/dot_general | solution.py:87
  305.2 0.7 fusion.54
  305.9 0.7 fusion.55
  306.7 0.3 reduce-window.9
  306.9 0.1 slice.68
  307.0 0.1 slice_reduce_fusion
  307.2 0.1 add_bitcast_fusion
  307.2 0.2 fusion.17
  307.4 0.2 select_reduce_fusion
  307.6 2.2 convolution_bitcast_fusion
  309.9 2.2 convolution_bitcast_fusion.1
  312.2 0.2 pad_maximum_fusion
  312.4 1.3 convolution_convert_fusion
  315.0 0.6 dynamic-slice
  316.3 0.3 dynamic-update-slice
  316.5 15.5 %all-reduce = s32[1536]{0:T(1024)S(1)} all-reduce(s32[1536]{0:T(1024)S(1)} %dynamic-update-slice), channel_id=1, replica_groups=mesh['walk'=8,'orb'=16] {'orb'}, use_global_device_ids=true, to_apply=%add | all-reduce | flops 1536 | bytes 12288
  332.1 1.3 slice.118
  333.4 4.8 %gather_fusion.1 = bf16[1536,256]{1,0:T(8,128)(2,1)S(1)} fusion(bf16[1024,256]{1,0:T(8,128)(2,1)S(1)} %slice.118, s32[2048]{0:T(1024)S(1)} %pad_clamp_fusion), kind=kCustom, calls=%fused_computation.1 | custom fusion | bytes 1579008 | tf_op jit(solution)/shard_map/while/body/eval_jaxpr/jit(_take)/gather | solution.py:128
  338.2 28.8 %all-gather.8.cloned.1.call-done = bf16[1536,1024]{1,0:T(8,128)(2,1)} async-done(((bf16[96,1024]{1,0:T(8,128)(2,1)}), bf16[1536,1024]{1,0:T(8,128)(2,1)}) %all-gather.8.cloned.1.call-update) | async-done | bytes 3145744 | tf_op jit(solution)/shard_map/while/body/eval_jaxpr/all_gather | solution.py:131
  367.0 3.8 fusion.12
  370.8 14.6 %all_to_all.5 = bf16[8,128,256]{2,1,0:T(8,128)(2,1)S(1)} all-to-all(bf16[8,128,256]{2,1,0:T(8,128)(2,1)S(1)} %bitcast.105), channel_id=1, replica_groups=mesh['walk'=8,'orb'=16] {'walk'}, dimensions={0} | all-to-all | bytes 1048576 | tf_op jit(solution)/shard_map/all_to_all | solution.py:31
  385.3 0.7 convert_reduce_fusion
  (56 shorter events, 1.2 us)
Async XLA Ops:
  6.5 4.8 %copy-start.3 = (s32[1,3,1024]{2,0,1:T(1,128)S(1)}, s32[1,3,1024]{2,0,1:T(1,128)}, u32[]{:S(2)}) copy-start(s32[1,3,1024]{2,0,1:T(1,128)} %param.11) | copy-start | bytes 36868
  6.5 5.6 %copy-start = (bf16[4096,256]{1,0:T(8,128)(2,1)S(1)}, bf16[4096,256]{1,0:T(8,128)(2,1)}, u32[]{:S(2)}) copy-start(bf16[4096,256]{1,0:T(8,128)(2,1)} %param.9) | copy-start | bytes 6291460
  6.5 301.1 %all-gather.6.cloned.1.call-start = ((), (), s32[]{:S(2)}) async-start(), calls=%async_computation.2 | async-start | bytes 1114112 | tf_op jit(solution)/shard_map/while/body/eval_jaxpr/all_gather | solution.py:19
  8.2 301.7 %all-gather.4.cloned.1.call-start = ((), (), s32[]{:S(2)}) async-start(), calls=%async_computation.1 | async-start | bytes 1114112 | tf_op jit(solution)/shard_map/while/body/eval_jaxpr/all_gather | solution.py:19
  9.0 358.0 %all-gather.8.cloned.1.call-start = ((), (), s32[]{:S(2)}) async-start(), calls=%async_computation.3 | async-start | bytes 3342336 | tf_op jit(solution)/shard_map/while/body/eval_jaxpr/all_gather | solution.py:131
  12.2 294.5 %copy-start.2 = (s32[1024]{0:T(1024)S(1)}, s32[1024]{0:T(1024)}, u32[]{:S(2)}) copy-start(s32[1024]{0:T(1024)} %param.15) | copy-start | bytes 12292
  312.1 2.9 copy-start.4
  312.4 19.7 %copy-start.1 = (f32[16,64,512]{2,1,0:T(8,128)}, f32[16,64,512]{2,1,0:T(8,128)S(1)}, u32[]{:S(2)}) copy-start(f32[16,64,512]{2,1,0:T(8,128)S(1)} %pad_maximum_fusion) | copy-start | bytes 6291460
Sparse Core Ops, SparseCore 0:
  9.8 47.2 all-gather.5
  59.6 43.6 all-gather.3
  313.8 53.1 all-gather.7
where the time goes:
time: 393 us
  local copies, waits for them, and re-layouts  272 us (69%)
  matrix products  35.4 us (9%)
  blocking collectives  30.1 us (8%)
  waiting for transfers between devices  29.6 us (8%)
  between operations  15.4 us (4%)
  other arithmetic  10.2 us (3%)
    gather x4, local copies, waits for them, and re-layouts, one_block(): gathered = jnp.take(coefficients, rows_one, axis=0)  259 us
    all_gather x1, waiting for transfers between devices, couple_slots(): lax.all_gather(slot_block, 'orb', axis=0, tiled=True)  28.8 us
    dot_general x4, matrix products, one_block(): jnp.einsum('nqk,nkw->nqw', weights_one, gathered, preferred_element_type=...  25.9 us
    unnamed x1, blocking collectives  15.5 us
    all_to_all x1, blocking collectives, summed_on_arrival(): blocks = lax.all_to_all(split_up(shard, dim, size), axis, 0, 0, tiled=True)  14.6 us
  transfers between devices with their start and end apart: 3, of which 1 were waited for; matrix products, arithmetic and copies ran while one was open for 78% of the time, Pallas kernels for 0%

commit v1 on v0

--- a/solution.py
+++ b/solution.py
@@ -4,6 +4,19 @@
 from jax.sharding import PartitionSpec as P
 
 GRID = 16
+
+
+def point_advance(s0, link_axis, join_dim):
+    long_array = jnp.concatenate(
+        jax.lax.all_to_all(
+            jnp.stack(jax.lax.psum(1, axis_name=link_axis) * [s0]),
+            axis_name=link_axis,
+            split_axis=0,
+            concat_axis=0,
+        ),
+        join_dim,
+    )
+    return long_array
 
 
 def joined_along(blocks, dim):
@@ -128,7 +141,7 @@
     ratio_rows = jnp.take(ratio, lax.all_gather(slot_rows, "orb", axis=0, tiled=True), axis=0)
     return jnp.einsum(
         "sn,sw->nw",
-        lax.all_gather(slot_block, "orb", axis=0, tiled=True),
+        point_advance(slot_block, "orb", 0),
         ratio_rows,
         preferred_element_type=jnp.float32,
     )

time: 393 us -> 406 us (1.033)
  waiting for transfers between devices: 29.6 us -> 0.74 us
  blocking collectives: 30.1 us -> 56.1 us
  starting transfers between devices: 0.08 us -> 8.21 us
    all_gather x1 -> x0, waiting for transfers between devices: 28.8 us -> none  [couple_slots(): lax.all_gather(slot_block, 'orb', axis=0, tiled=True)]
    unnamed x1, blocking collectives: 15.5 us -> 43.2 us
    all_to_all x0 -> x1, starting transfers between devices: none -> 8.17 us  [point_advance(): jax.lax.all_to_all(jnp.stack(jax.lax.psum(1, axis_name=link_axis) * [s0])...]
  transfers between devices with their start and end apart: 3 -> 3, of which waited for: 1 -> 0; matrix products, arithmetic and copies ran while one was open for 78% -> 77% of each run, Pallas kernels for 0% -> 0%
where the time goes in v1:
time: 406 us; the launch traced here: 402 us
  local copies, waits for them, and re-layouts  274 us (67%)
  blocking collectives  56.1 us (14%)
  matrix products  34.9 us (9%)
  between operations  15.6 us (4%)
  other arithmetic  12.5 us (3%)
  starting transfers between devices  8.21 us (2%)
    gather x4, local copies, waits for them, and re-layouts, one_block(): gathered = jnp.take(coefficients, rows_one, axis=0)  261 us
    unnamed x1, blocking collectives  43.2 us
    dot_general x4, matrix products, one_block(): jnp.einsum('nqk,nkw->nqw', weights_one, gathered, preferred_element_type=...  25.9 us
    all_to_all x1, blocking collectives, summed_on_arrival(): blocks = lax.all_to_all(split_up(shard, dim, size), axis, 0, 0, tiled=True)  13 us
    all_to_all x1, starting transfers between devices, point_advance(): jax.lax.all_to_all(jnp.stack(jax.lax.psum(1, axis_name=link_axis) * [s0])...  8.17 us
  transfers between devices with their start and end apart: 3, of which 0 were waited for; matrix products, arithmetic and copies ran while one was open for 77% of the time, Pallas kernels for 0%

profile of v1, /device:TPU:0, one launch (start us, length us, event | category | flops | bytes accessed | tf_op | source)
XLA Modules:
  0.0 402.3 jit_solution(5807631359581433649)
XLA Ops:
  6.5 1.7 fusion.39
  8.3 0.7 all-gather.3.cloned.1.call-update
  9.0 0.8 fusion.28
  9.8 0.8 broadcast_subtract_fusion.3
  10.9 0.1 add.378
  11.0 0.7 subtract_convert_fusion
  11.7 0.1 mul.535
  11.9 0.8 subtract_convert_fusion.1
  12.6 0.1 fusion.23
  12.8 0.1 add.399
  13.0 1.5 maximum_bitcast_fusion.1
  14.5 295.9 %while.17 = (s32[]{:T(128)}, bf16[4,256,512]{2,1,0:T(8,128)(2,1)}, bf16[4,256,4,64]{1,0,3,2:T(4,128)(2,1)S(1)}, s32[4,256,64]{1,0,2:T(4,128)S(1)}, bf16[4096,256]{1,0:T(8,128)(2,1)S(1)}, /*index=5*/s32[]{:T(128)}) while((s32[]{:T(128)}, bf16[4,256,512]{2,1,0:T(8,128)(2,1)}, bf16[4,256,4,64]{1,0,3,2:T(4,128)(2,1)S(1)}, ...), condition=%wide.region_1.2_spmd, body=%wide.region_0.1_spmd.sunk | while | flops 38699008 | bytes 30048844 | solution.py:109
  14.6 0.1 copy.28
  14.7 0.1 reshape.719
  14.8 65.2 %gather_fusion = bf16[16384,256]{1,0:T(8,128)(2,1)} fusion(bf16[4096,256]{1,0:T(8,128)(2,1)S(1)} %get-tuple-element.202, s32[16384]{0:T(1024)S(1)} %broadcast_clamp_fusion.2), kind=kCustom, calls=%fused_computation.clone.1 | custom fusion | bytes 16842752 | tf_op jit(solution)/shard_map/while/body/eval_jaxpr/while/body/eval_jaxpr/jit(_take)/gather | solution.py:99
  80.1 0.3 constant_dynamic-slice_fusion.5
  80.3 0.2 copy.29
  80.6 6.5 %fusion.53 = f32[256,4,256]{2,1,0:T(4,128)S(1)} fusion(bf16[256,64,256]{2,1,0:T(8,128)(2,1)} %bitcast.101, pred[256,64]{1,0:T(8,128)(4,1)S(1)} %compare_and_fusion.3, bf16[1,256,4,64]{3,2,1,0:T(4,128)(2,1)S(1)} %copy.29), kind=kOutput, calls=%fused_computation.2.clone.1 | convolution fusion | flops 37748736 | bytes 9584640 | tf_op jit(solution)/shard_map/while/body/eval_jaxpr/while/body/eval_jaxpr/nqk,nkw->nqw/dot_general | solution.py:100
  87.0 0.7 fusion.54
  87.8 0.7 fusion.55
  88.5 0.1 copy.28
  88.7 0.1 reshape.719
  88.8 65.2 %gather_fusion = bf16[16384,256]{1,0:T(8,128)(2,1)} fusion(bf16[4096,256]{1,0:T(8,128)(2,1)S(1)} %get-tuple-element.202, s32[16384]{0:T(1024)S(1)} %broadcast_clamp_fusion.2), kind=kCustom, calls=%fused_computation.clone.1 | custom fusion | bytes 16842752 | tf_op jit(solution)/shard_map/while/body/eval_jaxpr/while/body/eval_jaxpr/jit(_take)/gather | solution.py:99
  154.0 0.3 constant_dynamic-slice_fusion.5
  154.3 0.2 copy.29
  154.5 6.5 %fusion.53 = f32[256,4,256]{2,1,0:T(4,128)S(1)} fusion(bf16[256,64,256]{2,1,0:T(8,128)(2,1)} %bitcast.101, pred[256,64]{1,0:T(8,128)(4,1)S(1)} %compare_and_fusion.3, bf16[1,256,4,64]{3,2,1,0:T(4,128)(2,1)S(1)} %copy.29), kind=kOutput, calls=%fused_computation.2.clone.1 | convolution fusion | flops 37748736 | bytes 9584640 | tf_op jit(solution)/shard_map/while/body/eval_jaxpr/while/body/eval_jaxpr/nqk,nkw->nqw/dot_general | solution.py:100
  161.0 0.7 fusion.54
  161.7 0.7 fusion.55
  162.5 0.1 copy.28
  162.7 0.1 reshape.719
  162.8 65.2 %gather_fusion = bf16[16384,256]{1,0:T(8,128)(2,1)} fusion(bf16[4096,256]{1,0:T(8,128)(2,1)S(1)} %get-tuple-element.202, s32[16384]{0:T(1024)S(1)} %broadcast_clamp_fusion.2), kind=kCustom, calls=%fused_computation.clone.1 | custom fusion | bytes 16842752 | tf_op jit(solution)/shard_map/while/body/eval_jaxpr/while/body/eval_jaxpr/jit(_take)/gather | solution.py:99
  228.0 0.3 constant_dynamic-slice_fusion.5
  228.3 0.2 copy.29
  228.5 6.5 %fusion.53 = f32[256,4,256]{2,1,0:T(4,128)S(1)} fusion(bf16[256,64,256]{2,1,0:T(8,128)(2,1)} %bitcast.101, pred[256,64]{1,0:T(8,128)(4,1)S(1)} %compare_and_fusion.3, bf16[1,256,4,64]{3,2,1,0:T(4,128)(2,1)S(1)} %copy.29), kind=kOutput, calls=%fused_computation.2.clone.1 | convolution fusion | flops 37748736 | bytes 9584640 | tf_op jit(solution)/shard_map/while/body/eval_jaxpr/while/body/eval_jaxpr/nqk,nkw->nqw/dot_general | solution.py:100
  235.0 0.7 fusion.54
  235.7 0.7 fusion.55
  236.5 0.1 copy.28
  236.6 0.1 reshape.719
  236.8 65.2 %gather_fusion = bf16[16384,256]{1,0:T(8,128)(2,1)} fusion(bf16[4096,256]{1,0:T(8,128)(2,1)S(1)} %get-tuple-element.202, s32[16384]{0:T(1024)S(1)} %broadcast_clamp_fusion.2), kind=kCustom, calls=%fused_computation.clone.1 | custom fusion | bytes 16842752 | tf_op jit(solution)/shard_map/while/body/eval_jaxpr/while/body/eval_jaxpr/jit(_take)/gather | solution.py:99
  302.0 0.3 constant_dynamic-slice_fusion.5
  302.3 0.2 copy.29
  302.5 6.5 %fusion.53 = f32[256,4,256]{2,1,0:T(4,128)S(1)} fusion(bf16[256,64,256]{2,1,0:T(8,128)(2,1)} %bitcast.101, pred[256,64]{1,0:T(8,128)(4,1)S(1)} %compare_and_fusion.3, bf16[1,256,4,64]{3,2,1,0:T(4,128)(2,1)S(1)} %copy.29), kind=kOutput, calls=%fused_computation.2.clone.1 | convolution fusion | flops 37748736 | bytes 9584640 | tf_op jit(solution)/shard_map/while/body/eval_jaxpr/while/body/eval_jaxpr/nqk,nkw->nqw/dot_general | solution.py:100
  309.0 0.7 fusion.54
  309.7 0.7 fusion.55
  310.4 0.3 reduce-window.9
  310.7 0.1 slice.68
  310.8 0.1 slice_reduce_fusion
  310.9 0.1 add_bitcast_fusion
  311.0 0.2 fusion.17
  311.2 0.2 select_reduce_fusion
  311.4 3.2 convolution_bitcast_fusion
  314.6 2.3 convolution_bitcast_fusion.1
  317.0 0.2 pad_maximum_fusion
  317.2 0.3 convolution_convert_fusion
  317.5 2.1 stack.142
  319.6 8.2 %all-to-all-start = ((bf16[16,96,1024]{2,1,0:T(8,128)(2,1)}), bf16[16,96,1024]{2,1,0:T(8,128)(2,1)}, u32[]{:S(2)}, u32[]{:S(2)}) async-start(bf16[16,96,1024]{2,1,0:T(8,128)(2,1)} %stack.142), calls=%async_computation | async-start | bytes 6291456 | tf_op jit(solution)/shard_map/while/body/eval_jaxpr/all_to_all | solution.py:11
  329.0 0.6 dynamic-slice
  330.3 0.3 dynamic-update-slice
  330.6 43.2 %all-reduce = s32[1536]{0:T(1024)S(1)} all-reduce(s32[1536]{0:T(1024)S(1)} %dynamic-update-slice), channel_id=1, replica_groups=mesh['walk'=8,'orb'=16] {'orb'}, use_global_device_ids=true, to_apply=%add | all-reduce | flops 1536 | bytes 12288
  373.8 0.1 slice.118
  373.8 4.8 %gather_fusion.1 = bf16[1536,256]{1,0:T(8,128)(2,1)S(1)} fusion(bf16[1024,256]{1,0:T(8,128)(2,1)S(1)} %slice.118, s32[2048]{0:T(1024)S(1)} %pad_clamp_fusion), kind=kCustom, calls=%fused_computation.1 | custom fusion | bytes 1579008 | tf_op jit(solution)/shard_map/while/body/eval_jaxpr/jit(_take)/gather | solution.py:141
  378.6 3.2 fusion.12
  381.8 13.0 %all_to_all.11 = bf16[8,128,256]{2,1,0:T(8,128)(2,1)S(1)} all-to-all(bf16[8,128,256]{2,1,0:T(8,128)(2,1)S(1)} %bitcast.106), channel_id=1, replica_groups=mesh['walk'=8,'orb'=16] {'walk'}, dimensions={0} | all-to-all | bytes 1048576 | tf_op jit(solution)/shard_map/all_to_all | solution.py:44
  394.7 0.7 convert_reduce_fusion
  (56 shorter events, 1.2 us)
Async XLA Ops:
  6.5 6.1 %copy-start.3 = (s32[1,3,1024]{2,0,1:T(1,128)S(1)}, s32[1,3,1024]{2,0,1:T(1,128)}, u32[]{:S(2)}) copy-start(s32[1,3,1024]{2,0,1:T(1,128)} %param.11) | copy-start | bytes 36868
  6.5 7.9 %copy-start = (bf16[4096,256]{1,0:T(8,128)(2,1)S(1)}, bf16[4096,256]{1,0:T(8,128)(2,1)}, u32[]{:S(2)}) copy-start(bf16[4096,256]{1,0:T(8,128)(2,1)} %param.9) | copy-start | bytes 6291460
  6.5 304.9 %all-gather.5.cloned.1.call-start = ((), (), s32[]{:S(2)}) async-start(), calls=%async_computation.3 | async-start | bytes 1114112 | tf_op jit(solution)/shard_map/while/body/eval_jaxpr/all_gather | solution.py:32
  8.2 306.4 %all-gather.3.cloned.1.call-start = ((), (), s32[]{:S(2)}) async-start(), calls=%async_computation.2 | async-start | bytes 1114112 | tf_op jit(solution)/shard_map/while/body/eval_jaxpr/all_gather | solution.py:32
  14.5 295.9 %copy-start.2 = (s32[1024]{0:T(1024)S(1)}, s32[1024]{0:T(1024)}, u32[]{:S(2)}) copy-start(s32[1024]{0:T(1024)} %param.15) | copy-start | bytes 12292
  314.6 2.3 copy-start.1
  319.6 9.5 %copy-start.4 = (u32[128]{0:T(128)S(1)}, u32[128]{0:T(128)}, u32[]{:S(2)}) copy-start(u32[128]{0:T(128)} %constant.157) | copy-start | bytes 1540
  319.6 59.0 %all-to-all-start = ((bf16[16,96,1024]{2,1,0:T(8,128)(2,1)}), bf16[16,96,1024]{2,1,0:T(8,128)(2,1)}, u32[]{:S(2)}, u32[]{:S(2)}) async-start(bf16[16,96,1024]{2,1,0:T(8,128)(2,1)} %stack.142), calls=%async_computation | async-start | bytes 6291456 | tf_op jit(solution)/shard_map/while/body/eval_jaxpr/all_to_all | solution.py:11
Sparse Core Ops, SparseCore 0:
  9.8 47.2 all-gather.4
  59.6 43.6 all-gather.2
